TPU v7x, 32 devices: a whole 2x2x4 slice. The times are simulated.
32 devices in a mesh: blk: 8 (over y, x, core), grp: 4 (over z).
Axes of the slice: x: 2, y: 2, z: 4, core: 2. Of those that a mesh axis runs over, the one named last changes fastest.
Arguments:
- amplitudes: bfloat16 [896, 4, 896], P('blk', None, 'grp'), may hold values from -6 to 6
- grid_factor: bfloat16 [1024, 896], P(('blk', 'grp')), may hold values from -0.1875 to 0.1875
- metric: float32 [1024, 4, 256], P('blk', 'grp'), may hold values from -6 to 6
- virt_energy: float32 [896], replicated, may hold values from 0.2 to 4
- pair_energy: float32 [4], replicated, may hold values from -2 to -0.5
Outputs:
- residual: float32 [896, 4, 896], P('blk', None, 'grp')
All inputs are finite; a program needn't handle non-finite values.
Results may differ from a plain program's by a relative error of at most 0.005.
Values may be sent and summed in bfloat16 or wider, within the bound.
A program may use at most 64 MiB of HBM per device.

v0:
```python
import jax
import jax.numpy as jnp
from jax import lax
from jax.sharding import PartitionSpec as P


def local(amplitudes, grid_factor, metric, virt_energy, pair_energy):
    row_factor = lax.all_gather(grid_factor, "grp", axis=0, tiled=True)
    column_factor = lax.all_gather(grid_factor, "blk", axis=0, tiled=True)
    amplitude_rows = lax.all_gather(amplitudes, "blk", axis=0, tiled=True)
    row_count = row_factor.shape[0]
    left_part = jnp.einsum(
        "pc,ckd->kpd", row_factor, amplitude_rows, preferred_element_type=jnp.float32
    ).astype(jnp.bfloat16)
    columns = column_factor
    products = jnp.einsum(
        "kpd,qd->kpq",
        lax.all_gather(left_part, "grp", axis=2, tiled=True),
        columns,
        preferred_element_type=jnp.float32,
    )
    weighted = (metric.reshape(row_count, -1)[None] * products).astype(jnp.bfloat16)
    columns = column_factor
    mixed = lax.psum_scatter(
        jnp.einsum("kpq,qb->bkp", weighted, columns, preferred_element_type=jnp.float32).astype(
            jnp.bfloat16
        ),
        "grp",
        scatter_dimension=0,
        tiled=True,
    )
    columns = row_factor
    ladder = lax.psum_scatter(
        jnp.einsum("pa,bkp->akb", columns, mixed, preferred_element_type=jnp.float32).astype(
            jnp.bfloat16
        ),
        "blk",
        scatter_dimension=0,
        tiled=True,
    ).astype(jnp.float32)
    first_energy = lax.dynamic_slice_in_dim(
        virt_energy, lax.axis_index("blk") * amplitudes.shape[0], amplitudes.shape[0]
    )
    second_energy = lax.dynamic_slice_in_dim(
        virt_energy, lax.axis_index("grp") * amplitudes.shape[2], amplitudes.shape[2]
    )
    denominator = (
        first_energy[:, None, None] + second_energy[None, None, :] - pair_energy[None, :, None]
    )
    return denominator * amplitudes.astype(jnp.float32) + ladder


def solution(mesh):
    in_specs = (P("blk", None, "grp"), P(("blk", "grp"), None), P("blk", "grp", None), P(), P())
    out_specs = P("blk", None, "grp")
    return jax.shard_map(local, mesh=mesh, in_specs=in_specs, out_specs=out_specs, check_vma=False)
```

profile of v0, /device:TPU:25, one launch (start us, length us, event | category | flops | bytes accessed | tf_op | source)
XLA Modules:
  0.0 137.0 jit_solution(9741608353748779387)
XLA Ops:
  6.5 0.0 all-gather.2.cloned.1.call-start
  6.5 0.7 all-gather.2.cloned.1.call-update
  7.3 0.0 reduce-scatter.5.cloned.1.call-start
  7.3 0.9 copy.23
  8.2 11.1 %all_gather.13 = bf16[128,896]{1,0:T(8,128)(2,1)S(1)} all-gather(bf16[32,896]{1,0:T(8,128)(2,1)} %param.6), channel_id=1, replica_groups=mesh['blk'=8,'grp'=4] {'grp'}, dimensions={0}, use_global_device_ids=true | all-gather | bytes 286720 | tf_op jit(solution)/shard_map/all_gather | solution.py:8
  19.3 14.9 %all_gather.15 = bf16[256,896]{1,0:T(8,128)(2,1)S(1)} all-gather(bf16[32,896]{1,0:T(8,128)(2,1)} %param.6), channel_id=1, replica_groups=mesh['blk'=8,'grp'=4] {'blk'}, dimensions={0}, use_global_device_ids=true | all-gather | bytes 516096 | tf_op jit(solution)/shard_map/all_gather | solution.py:9
  34.2 3.7 %all-gather.2.cloned.1.call-done = bf16[896,4,224]{2,1,0:T(4,128)(2,1)} async-done(((bf16[112,4,224]{2,1,0:T(4,128)(2,1)}), bf16[896,4,224]{2,1,0:T(4,128)(2,1)}) %all-gather.2.cloned.1.call-update) | async-done | bytes 1605648 | tf_op jit(solution)/shard_map/all_gather | solution.py:10
  37.9 2.2 %fusion.7 = bf16[4,128,224]{1,2,0:T(8,128)(2,1)S(1)} fusion(bf16[896,4,224]{2,1,0:T(4,128)(2,1)} %all-gather.2.cloned.1.call-done, bf16[128,896]{1,0:T(8,128)(2,1)S(1)} %all_gather.13), kind=kOutput, calls=%fused_computation.8 | convolution fusion | flops 205635584 | bytes 2064384 | tf_op jit(solution)/shard_map/pc,ckd->kpd/dot_general | solution.py:12
  40.1 19.2 %all_gather.14 = bf16[4,128,896]{1,2,0:T(8,128)(2,1)S(1)} all-gather(bf16[4,128,224]{1,2,0:T(8,128)(2,1)S(1)} %fusion.7), channel_id=1, replica_groups=mesh['blk'=8,'grp'=4] {'grp'}, dimensions={2}, use_global_device_ids=true | all-gather | bytes 1146880 | tf_op jit(solution)/shard_map/all_gather | solution.py:18
  59.3 2.2 %fusion.2 = bf16[896,4,128]{2,0,1:T(8,128)(2,1)} fusion(bf16[4,128,896]{1,2,0:T(8,128)(2,1)S(1)} %all_gather.14, bf16[256,896]{1,0:T(8,128)(2,1)S(1)} %all_gather.15, f32[128,256]{1,0:T(8,128)S(1)} %bitcast.25), kind=kOutput, calls=%fused_computation.4 | convolution fusion | flops 470482944 | bytes 2424832 | tf_op jit(solution)/shard_map/kpq,qb->bkp/dot_general | solution.py:25
  61.5 0.0 reduce-scatter.5.cloned.1.call-update
  61.5 0.0 reduce-scatter.7.cloned.1.call-start
  61.6 22.9 %reduce-scatter.5.cloned.1.call-done = bf16[224,4,128]{2,0,1:T(8,128)(2,1)} async-done(((bf16[896,4,128]{2,0,1:T(8,128)(2,1)}), bf16[224,4,128]{2,0,1:T(8,128)(2,1)}) %reduce-scatter.5.cloned.1.call-update) | async-done | bytes 229392 | tf_op jit(solution)/shard_map/reduce_scatter | solution.py:24
  84.5 1.5 %convolution_convert_fusion = bf16[224,4,896]{2,0,1:T(8,128)(2,1)S(1)} fusion(bf16[224,4,128]{2,0,1:T(8,128)(2,1)} %reduce-scatter.5.cloned.1.call-done, bf16[128,896]{1,0:T(8,128)(2,1)S(1)} %all_gather.13), kind=kOutput, calls=%fused_computation.2 | convolution fusion | flops 206323712 | bytes 2064384 | tf_op jit(solution)/shard_map/pa,bkp->akb/dot_general | solution.py:34
  86.0 0.0 copy-start
  86.0 2.3 %copy.13 = bf16[896,896]{1,0:T(8,128)(2,1)} copy(bf16[896,896]{0,1:T(8,128)(2,1)S(1)} %bitcast.23) | data formatting | bytes 3211264
  88.3 0.0 copy-start.1
  88.3 0.0 reduce-scatter.7.cloned.1.call-update
  88.3 0.0 copy-done
  88.3 0.2 copy.8
  88.6 0.8 dynamic_slice.7
  89.3 0.8 dynamic_slice.6
  90.1 0.1 broadcast_add_fusion
  90.2 38.1 %reduce-scatter.7.cloned.1.call-done = bf16[112,896]{1,0:T(8,128)(2,1)} async-done(((bf16[896,896]{1,0:T(8,128)(2,1)}), bf16[112,896]{1,0:T(8,128)(2,1)}) %reduce-scatter.7.cloned.1.call-update) | async-done | bytes 200720
  128.2 1.1 copy.14
  129.3 0.0 copy-done.1
  129.4 0.2 convert_add_fusion
  129.5 1.0 copy.9
Async XLA Ops:
  6.5 31.4 %all-gather.2.cloned.1.call-start = ((), (), s32[]{:S(2)}) async-start(), calls=%async_computation.2 | async-start | bytes 2064384 | tf_op jit(solution)/shard_map/all_gather | solution.py:10
  7.3 77.2 %reduce-scatter.5.cloned.1.call-start = ((), (), s32[]{:S(2)}) async-start(), calls=%async_computation.3 | async-start | bytes 1146880 | tf_op jit(solution)/shard_map/reduce_scatter | solution.py:24
  61.5 66.7 %reduce-scatter.7.cloned.1.call-start = ((), (), s32[]{:S(2)}) async-start(), calls=%async_computation.4 | async-start | bytes 1806336
  86.0 2.4 %copy-start = (bf16[112,4,224]{2,1,0:T(4,128)(2,1)S(1)}, bf16[112,4,224]{2,1,0:T(4,128)(2,1)}, u32[]{:S(2)}) copy-start(bf16[112,4,224]{2,1,0:T(4,128)(2,1)} %param.5) | copy-start | bytes 602116
  88.3 41.0 %copy-start.1 = (f32[4]{0:T(128)S(1)}, f32[4]{0:T(128)}, u32[]{:S(2)}) copy-start(f32[4]{0:T(128)} %param.9) | copy-start | bytes 52
Sparse Core Ops, SparseCore 0:
  9.2 28.6 all-gather.1
  61.6 22.8 reduce-scatter.4
  88.5 39.7 reduce-scatter.6
where the time goes:
time: 139 us; the launch traced here: 137 us
  waiting for transfers between devices  65.4 us (47%)
  blocking collectives  45.1 us (32%)
  between operations  13.2 us (9%)
  local copies, waits for them, and re-layouts  7.03 us (5%)
  matrix products  5.91 us (4%)
    unnamed x4, waiting for transfers between devices  38.8 us
    reduce_scatter x1, waiting for transfers between devices, local(): lax.psum_scatter(jnp.einsum('kpq,qb->bkp', weighted, columns, preferred_e...  22.9 us
    all_gather x1, blocking collectives, local(): lax.all_gather(left_part, 'grp', axis=2, tiled=True)  19.2 us
    all_gather x1, blocking collectives, local(): column_factor = lax.all_gather(grid_factor, 'blk', axis=0, tiled=True)  14.9 us
    all_gather x1, blocking collectives, local(): row_factor = lax.all_gather(grid_factor, 'grp', axis=0, tiled=True)  11.1 us
    unnamed x8, local copies, waits for them, and re-layouts  4.55 us
    all_gather x1, waiting for transfers between devices, local(): amplitude_rows = lax.all_gather(amplitudes, 'blk', axis=0, tiled=True)  3.7 us
  transfers between devices with their start and end apart: 3, of which 3 were waited for; matrix products, arithmetic and copies ran while one was open for 2% of the time, Pallas kernels for 0%

commit v1 on v0

--- a/solution.py
+++ b/solution.py
@@ -1,6 +1,10 @@
+import functools
+
 import jax
 import jax.numpy as jnp
 from jax import lax
+from jax.experimental import pallas as pl
+from jax.experimental.pallas import tpu as pltpu
 from jax.sharding import PartitionSpec as P
 
 
@@ -50,7 +54,262 @@
     return denominator * amplitudes.astype(jnp.float32) + ladder
 
 
+MESH = pl.DeviceIdType.MESH
+F32 = jnp.float32
+BF16 = jnp.bfloat16
+
+
+def flip(index, mask):
+    bit = 1
+    while bit <= mask:
+        if mask & bit:
+            index = index + bit - 2 * bit * lax.rem(lax.div(index, bit), 2)
+        bit *= 2
+    return index
+
+
+def column_chunks(total, width):
+    return [(start, min(width, total - start)) for start in range(0, total, width)]
+
+
+def kernel(
+    n_blk, n_grp, t_ref, x_ref, z_ref, o_ref,
+    factor, pieces, amps, weights, left, mixed, ladder, out_send, out_recv,
+    z_send_sem, z_recv_sem, p_send_sem, p_recv_sem, o_send_sem, o_recv_sem,
+):
+    me = lax.axis_index("blk")
+    grp = lax.axis_index("grp")
+    pairs, rows, cols = t_ref.shape
+    points, virtuals = x_ref.shape
+    even = list(range(2, n_blk, 2))
+    direct = even + [1]
+    started = []
+
+    def peer(step):
+        return lax.rem(grp + step, n_grp)
+
+    barrier = pltpu.get_barrier_semaphore()
+    for step in range(1, n_grp):
+        pl.semaphore_signal(barrier, inc=1, device_id={"grp": peer(step)}, device_id_type=MESH)
+    for mask in direct:
+        pl.semaphore_signal(barrier, inc=1, device_id={"blk": flip(me, mask)}, device_id_type=MESH)
+    pl.semaphore_wait(barrier, n_grp - 1 + len(direct))
+
+    def rows_of(source, size):
+        return pl.ds(pl.multiple_of(source * size, size), size)
+
+    def z_copy(kind, step, src, dst):
+        return pltpu.make_async_remote_copy(
+            src_ref=src, dst_ref=dst,
+            send_sem=z_send_sem.at[kind, step], recv_sem=z_recv_sem.at[kind, step],
+            device_id={"grp": peer(step)}, device_id_type=MESH,
+        )
+
+    def z_dst(kind, source):
+        if kind == 0:
+            return factor.at[source, rows_of(me, points), :]
+        return (pieces if kind == 1 else weights).at[source]
+
+    def z_start(kind, step):
+        src = (x_ref, t_ref.at[peer(step)], z_ref)[kind]
+        copy = z_copy(kind, step, src, z_dst(kind, grp))
+        copy.start()
+        started.append(copy)
+
+    def z_wait(kind, step):
+        dst = z_dst(kind, peer(n_grp - step))
+        z_copy(kind, step, dst, dst).wait_recv()
+
+    chunks = column_chunks(virtuals, -(-cols // 128) * 128)
+
+    def region(item, source):
+        if item < n_grp:
+            return factor.at[peer((n_grp - item) % n_grp), rows_of(source, points), :]
+        if item == n_grp:
+            return amps.at[rows_of(source, rows), :]
+        start, width = chunks[item - n_grp - 1]
+        return mixed.at[:, rows_of(source, points), pl.ds(start, width)]
+
+    def p_copy(item, mask, hop, src=None):
+        place = region(item, flip(me, mask))
+        return pltpu.make_async_remote_copy(
+            src_ref=place if src is None else src, dst_ref=place,
+            send_sem=p_send_sem.at[item, mask ^ hop], recv_sem=p_recv_sem.at[item, mask ^ hop],
+            device_id={"blk": flip(me, hop)}, device_id_type=MESH,
+        )
+
+    def p_wait(item, mask):
+        place = region(item, flip(me, mask))
+        pltpu.make_async_remote_copy(
+            src_ref=place, dst_ref=place,
+            send_sem=p_send_sem.at[item, mask], recv_sem=p_recv_sem.at[item, mask],
+            device_id={"blk": flip(me, mask)}, device_id_type=MESH,
+        ).wait_recv()
+
+    def p_spread(item, src=None):
+        for mask in direct:
+            copy = p_copy(item, 0, mask, src)
+            copy.start()
+            started.append(copy)
+
+    def p_forward(item):
+        for mask in even:
+            p_wait(item, mask)
+            copy = p_copy(item, mask, 1)
+            copy.start()
+            started.append(copy)
+
+    def p_rest(item):
+        for mask in range(1, n_blk, 2):
+            p_wait(item, mask)
+
+    for step in range(1, n_grp):
+        z_start(0, step)
+    p_spread(0, x_ref)
+    for kind in (1, 2):
+        for step in range(1, n_grp):
+            z_start(kind, step)
+    factor[grp, rows_of(me, points), :] = x_ref[...]
+    pieces[grp] = t_ref[grp]
+    weights[grp] = z_ref[...]
+    for step in range(1, n_grp):
+        z_wait(0, step)
+        p_spread(step)
+    for step in range(1, n_grp):
+        z_wait(1, step)
+    for g in range(n_grp):
+        amps[rows_of(me, rows), g * cols:(g + 1) * cols] = pieces[g]
+    p_spread(n_grp)
+    for item in range(n_grp + 1):
+        p_forward(item)
+    for item in range(n_grp + 1):
+        p_rest(item)
+    for step in range(1, n_grp):
+        z_wait(2, step)
+
+    own = factor[:, rows_of(me, points), :].reshape(n_grp * points, virtuals)
+    left[...] = jnp.dot(own, amps[...], preferred_element_type=F32).astype(BF16)
+    weighted = []
+    for g in range(n_grp):
+        products = lax.dot_general(
+            left[...], factor[g], (((1,), (1,)), ((), ())), preferred_element_type=F32
+        )
+        weighted.append((weights[g].astype(F32) * products).astype(BF16))
+    weighted = jnp.concatenate(weighted, axis=1)
+    total = n_grp * n_blk * points
+    for number, (start, width) in enumerate(chunks):
+        part = jnp.dot(
+            weighted, factor[:, :, start:start + width].reshape(total, width),
+            preferred_element_type=F32,
+        ).astype(BF16)
+        mixed[:, rows_of(me, points), start:start + width] = part.reshape(n_grp, points, width)
+        p_spread(n_grp + 1 + number)
+
+    picked = lax.broadcasted_iota(jnp.int32, (rows, virtuals), 1) == (
+        lax.broadcasted_iota(jnp.int32, (rows, virtuals), 0) + me * rows
+    )
+    picked = picked.astype(F32).astype(BF16)
+    columns = lax.dot_general(
+        picked, factor[...].reshape(total, virtuals), (((1,), (1,)), ((), ())),
+        preferred_element_type=F32,
+    ).astype(BF16)
+
+    def o_copy(target, source):
+        return pltpu.make_async_remote_copy(
+            src_ref=out_send.at[target], dst_ref=out_recv.at[source],
+            send_sem=o_send_sem.at[target], recv_sem=o_recv_sem.at[source],
+            device_id={"grp": target}, device_id_type=MESH,
+        )
+
+    done = 0
+    for number, (start, width) in enumerate(chunks):
+        p_forward(n_grp + 1 + number)
+        p_rest(n_grp + 1 + number)
+        ladder[:, start:start + width] = jnp.dot(
+            columns, mixed[:, :, start:start + width].reshape(total, width),
+            preferred_element_type=F32,
+        )
+        while done < n_grp and (done + 1) * cols <= start + width:
+            block = ladder[:, done * cols:(done + 1) * cols].astype(BF16)
+            out_send[done] = block
+
+            @pl.when(grp != done)
+            def _(target=done):
+                o_copy(target, grp).start()
+
+            done += 1
+    for step in range(1, n_grp):
+        source = peer(step)
+        o_copy(source, source).wait_recv()
+        o_ref[source] = out_recv[source]
+    o_ref[grp] = out_send[grp]
+    for target in range(n_grp):
+        @pl.when(grp != target)
+        def _(target=target):
+            o_copy(target, grp).wait_send()
+    for copy in started:
+        copy.wait_send()
+
+
+def ladder_term(n_blk, n_grp, amps, factor_rows, weights):
+    pairs, rows, cols = amps.shape
+    points, virtuals = factor_rows.shape
+    items = n_grp + 1 + len(column_chunks(virtuals, -(-cols // 128) * 128))
+    dma = pltpu.SemaphoreType.DMA
+    vmem = pl.BlockSpec(memory_space=pltpu.VMEM)
+    return pl.pallas_call(
+        functools.partial(kernel, n_blk, n_grp),
+        out_shape=jax.ShapeDtypeStruct(amps.shape, BF16),
+        in_specs=[vmem] * 3,
+        out_specs=vmem,
+        scratch_shapes=[
+            pltpu.VMEM((n_grp, n_blk * points, virtuals), BF16),
+            pltpu.VMEM((n_grp, rows, cols), BF16),
+            pltpu.VMEM((n_blk * rows, virtuals), BF16),
+            pltpu.VMEM((n_grp,) + weights.shape, BF16),
+            pltpu.VMEM((n_grp * points, virtuals), BF16),
+            pltpu.VMEM((n_grp, n_blk * points, virtuals), BF16),
+            pltpu.VMEM((rows, virtuals), F32),
+            pltpu.VMEM((n_grp, rows, cols), BF16),
+            pltpu.VMEM((n_grp, rows, cols), BF16),
+            dma((3, n_grp)), dma((3, n_grp)),
+            dma((items, n_blk)), dma((items, n_blk)),
+            dma((n_grp,)), dma((n_grp,)),
+        ],
+        compiler_params=pltpu.CompilerParams(collective_id=0, has_side_effects=True),
+    )(amps, factor_rows, weights)
+
+
+def denominators(amplitudes, virt_energy, pair_energy):
+    first_energy = lax.dynamic_slice_in_dim(
+        virt_energy, lax.axis_index("blk") * amplitudes.shape[0], amplitudes.shape[0]
+    )
+    second_energy = lax.dynamic_slice_in_dim(
+        virt_energy, lax.axis_index("grp") * amplitudes.shape[2], amplitudes.shape[2]
+    )
+    return first_energy[:, None, None] + second_energy[None, None, :] - pair_energy[None, :, None]
+
+
+def by_pair(n_blk, n_grp, amplitudes, grid_factor, metric, virt_energy, pair_energy):
+    ladder = ladder_term(
+        n_blk, n_grp, jnp.transpose(amplitudes, (1, 0, 2)), grid_factor, metric[:, 0].astype(BF16)
+    )
+    denominator = denominators(amplitudes, virt_energy, pair_energy)
+    return denominator * amplitudes.astype(F32) + jnp.transpose(ladder, (1, 0, 2)).astype(F32)
+
+
 def solution(mesh):
     in_specs = (P("blk", None, "grp"), P(("blk", "grp"), None), P("blk", "grp", None), P(), P())
     out_specs = P("blk", None, "grp")
-    return jax.shard_map(local, mesh=mesh, in_specs=in_specs, out_specs=out_specs, check_vma=False)
+    n_blk, n_grp = mesh.shape["blk"], mesh.shape["grp"]
+
+    def body(amplitudes, *rest):
+        rows, pairs, cols = amplitudes.shape
+        points, virtuals = rest[0].shape
+        fits = pairs == n_grp and n_blk & (n_blk - 1) == 0 and n_blk >= 4
+        fits = fits and rows % 16 == 0 and points % 16 == 0 and virtuals % 128 == 0
+        if fits:
+            return by_pair(n_blk, n_grp, amplitudes, *rest)
+        return local(amplitudes, *rest)
+
+    return jax.shard_map(body, mesh=mesh, in_specs=in_specs, out_specs=out_specs, check_vma=False)

time: 139 us -> 56.8 us (0.41)
  waiting for transfers between devices: 65.4 us -> 0 us
  Pallas kernels: 0 us -> 49.6 us
  blocking collectives: 45.1 us -> 0 us
  between operations: 13.2 us -> 0.04 us
  matrix products: 5.91 us -> 0 us
  local copies, waits for them, and re-layouts: 7.03 us -> 4.87 us
    pallas_call x0 -> x1, Pallas kernels: none -> 49.6 us  [ladder_term(): pl.pallas_call(functools.partial(kernel, n_blk, n_grp), out_shape=jax.Sha...]
    all_gather x3 -> x0, blocking collectives: 45.1 us -> none  [the longest x1 19.2 us: local(): lax.all_gather(left_part, 'grp', axis=2, tiled=True)]
    unnamed x4 -> x0, waiting for transfers between devices: 38.8 us -> none
    reduce_scatter x1 -> x0, waiting for transfers between devices: 22.9 us -> none  [local(): lax.psum_scatter(jnp.einsum('kpq,qb->bkp', weighted, columns, preferred_e...]
    dot_general x3 -> x0, matrix products: 5.91 us -> none  [the longest x1 2.23 us: local(): jnp.einsum('pc,ckd->kpd', row_factor, amplitude_rows, preferred_element_t...]
    all_gather x1 -> x0, waiting for transfers between devices: 3.7 us -> none  [local(): amplitude_rows = lax.all_gather(amplitudes, 'blk', axis=0, tiled=True)]
    unnamed x8 -> x6, local copies, waits for them, and re-layouts: 4.55 us -> 2.25 us
  transfers between devices with their start and end apart: 3 -> 0, of which waited for: 3 -> 0; matrix products, arithmetic and copies ran while one was open for 2% -> 0% of each run, Pallas kernels for 0% -> 0%
where the time goes in v1:
time: 56.8 us; the launch traced here: 55.7 us
  Pallas kernels  49.6 us (87%)
  local copies, waits for them, and re-layouts  4.87 us (9%)
  other arithmetic  1.16 us (2%)
    pallas_call x1, Pallas kernels, ladder_term(): pl.pallas_call(functools.partial(kernel, n_blk, n_grp), out_shape=jax.Sha...  49.6 us
    unnamed x6, local copies, waits for them, and re-layouts  2.25 us

profile of v1, /device:TPU:25, one launch (start us, length us, event | category | flops | bytes accessed | tf_op | source)
XLA Modules:
  0.0 55.7 jit_solution(17544899449395125959)
XLA Ops:
  0.0 0.0 copy-start
  0.0 0.8 %dynamic_slice.6 = f32[112]{0:T(128)S(1)} dynamic-slice(f32[896]{0:T(1024)} %param.8, s32[]{:T(128)S(6)} %select_n.6), dynamic_slice_sizes={112} | dynamic-slice | bytes 900 | tf_op jit(solution)/shard_map/dynamic_slice | solution.py:284
  0.8 0.8 %dynamic_slice.7 = f32[224]{0:T(256)S(1)} dynamic-slice(f32[896]{0:T(1024)} %param.8, s32[]{:T(128)S(6)} %select_n.7), dynamic_slice_sizes={224} | dynamic-slice | bytes 1796 | tf_op jit(solution)/shard_map/dynamic_slice | solution.py:287
  1.6 1.5 %copy.16 = bf16[128,1,256]{2,0,1:T(8,128)(2,1)} copy(f32[128,1,256]{2,1,0:T(1,128)} %param.7) | data formatting | bytes 196608 | tf_op args[2]
  3.1 0.1 broadcast_add_fusion
  3.2 0.0 copy-done
  3.2 0.7 %copy.15 = bf16[112,4,224]{2,0,1:T(8,128)(2,1)} copy(bf16[112,4,224]{2,1,0:T(4,128)(2,1)S(1)} %copy-done) | data formatting | bytes 401408 | tf_op args[0]
  3.9 0.0 copy-start.1
  3.9 49.6 %shard_map.55 = bf16[4,112,224]{2,1,0:T(8,128)(2,1)} custom-call(bf16[4,112,224]{2,1,0:T(8,128)(2,1)} %bitcast.8, bf16[32,896]{1,0:T(8,128)(2,1)} %x_ref.1, bf16[128,256]{1,0:T(8,128)(2,1)} %bitcast.9), custom_call_target="tpu_custom_call" | custom-call | tf_op jit(solution)/shard_map/pallas_call | solution.py:260
  53.5 0.0 copy-done.1
  53.5 1.1 %bitcast_add_fusion = f32[112,4,224]{2,0,1:T(8,128)S(1)} fusion(bf16[4,112,224]{2,1,0:T(8,128)(2,1)} %shard_map.55, f32[4]{0:T(128)S(1)} %copy-done.1, f32[112,224]{1,0:T(8,128)S(1)} %broadcast_add_fusion, bf16[112,4,224]{2,1,0:T(4,128)(2,1)S(1)} %copy-done), kind=kLoop, calls=%fused_computation | loop fusion | flops 501760 | bytes 903184 | tf_op jit(solution)/shard_map/add | solution.py:298
  54.6 1.1 %copy.9 = f32[112,4,224]{2,1,0:T(4,128)} copy(f32[112,4,224]{2,0,1:T(8,128)S(1)} %bitcast_add_fusion) | data formatting | bytes 802816 | tf_op jit(solution)/shard_map/add | solution.py:298
Async XLA Ops:
  0.0 3.2 %copy-start = (bf16[112,4,224]{2,1,0:T(4,128)(2,1)S(1)}, bf16[112,4,224]{2,1,0:T(4,128)(2,1)}, u32[]{:S(2)}) copy-start(bf16[112,4,224]{2,1,0:T(4,128)(2,1)} %param.5) | copy-start | bytes 602116
  3.9 49.6 %copy-start.1 = (f32[4]{0:T(128)S(1)}, f32[4]{0:T(128)}, u32[]{:S(2)}) copy-start(f32[4]{0:T(128)} %param.9) | copy-start | bytes 52

commit v2 on v1

--- a/solution.py
+++ b/solution.py
@@ -81,8 +81,8 @@
     grp = lax.axis_index("grp")
     pairs, rows, cols = t_ref.shape
     points, virtuals = x_ref.shape
-    even = list(range(2, n_blk, 2))
-    direct = even + [1]
+    core, near, far = 1, 2, 4
+    direct = [near, far, core]
     started = []
 
     def peer(step):
@@ -122,46 +122,65 @@
 
     chunks = column_chunks(virtuals, -(-cols // 128) * 128)
 
-    def region(item, source):
+    def region(item, half, source):
         if item < n_grp:
-            return factor.at[peer((n_grp - item) % n_grp), rows_of(source, points), :]
+            part = points // 2
+            begin = pl.multiple_of(source * points + half * part, part)
+            return factor.at[peer((n_grp - item) % n_grp), pl.ds(begin, part), :]
         if item == n_grp:
-            return amps.at[rows_of(source, rows), :]
+            part = -(-rows // 32) * 16
+            size = part if half == 0 else rows - part
+            begin = pl.multiple_of(source * rows + half * part, 16)
+            return amps.at[pl.ds(begin, size), :]
         start, width = chunks[item - n_grp - 1]
-        return mixed.at[:, rows_of(source, points), pl.ds(start, width)]
-
-    def p_copy(item, mask, hop, src=None):
-        place = region(item, flip(me, mask))
+        part = n_grp // 2
+        return mixed.at[pl.ds(half * part, part), rows_of(source, points), pl.ds(start, width)]
+
+    def p_copy(item, half, mask, hop, src=None):
+        place = region(item, half, flip(me, mask))
         return pltpu.make_async_remote_copy(
             src_ref=place if src is None else src, dst_ref=place,
-            send_sem=p_send_sem.at[item, mask ^ hop], recv_sem=p_recv_sem.at[item, mask ^ hop],
+            send_sem=p_send_sem.at[item, half, mask ^ hop],
+            recv_sem=p_recv_sem.at[item, half, mask ^ hop],
             device_id={"blk": flip(me, hop)}, device_id_type=MESH,
         )
 
-    def p_wait(item, mask):
-        place = region(item, flip(me, mask))
-        pltpu.make_async_remote_copy(
-            src_ref=place, dst_ref=place,
-            send_sem=p_send_sem.at[item, mask], recv_sem=p_recv_sem.at[item, mask],
-            device_id={"blk": flip(me, mask)}, device_id_type=MESH,
-        ).wait_recv()
+    def p_send(item, half, mask, hop, src=None):
+        copy = p_copy(item, half, mask, hop, src)
+        copy.start()
+        started.append(copy)
+
+    def p_wait(item, half, mask):
+        p_copy(item, half, mask, 0).wait_recv()
 
     def p_spread(item, src=None):
-        for mask in direct:
-            copy = p_copy(item, 0, mask, src)
-            copy.start()
-            started.append(copy)
-
-    def p_forward(item):
-        for mask in even:
-            p_wait(item, mask)
-            copy = p_copy(item, mask, 1)
-            copy.start()
-            started.append(copy)
+        sources = (None, None)
+        if src is not None:
+            part = points // 2
+            sources = tuple(src.at[half * part:(half + 1) * part, :] for half in range(2))
+        for turn in range(2):
+            p_send(item, turn, 0, near, sources[turn])
+            p_send(item, 1 - turn, 0, far, sources[1 - turn])
+        for half in range(2):
+            p_send(item, half, 0, core, sources[half])
+
+    def p_relay(item):
+        for turn in range(2):
+            for mask, half, onward in ((near, turn, far), (far, 1 - turn, near)):
+                p_wait(item, half, mask)
+                if turn == 0:
+                    p_send(item, half, mask, onward)
+                p_send(item, half, mask, core)
+
+    def p_across(item):
+        for half in range(2):
+            p_wait(item, half, near + far)
+            p_send(item, half, near + far, core)
 
     def p_rest(item):
         for mask in range(1, n_blk, 2):
-            p_wait(item, mask)
+            for half in range(2):
+                p_wait(item, half, mask)
 
     for step in range(1, n_grp):
         z_start(0, step)
@@ -175,13 +194,17 @@
     for step in range(1, n_grp):
         z_wait(0, step)
         p_spread(step)
+        p_relay(step - 1)
+    p_relay(n_grp - 1)
     for step in range(1, n_grp):
         z_wait(1, step)
     for g in range(n_grp):
         amps[rows_of(me, rows), g * cols:(g + 1) * cols] = pieces[g]
     p_spread(n_grp)
-    for item in range(n_grp + 1):
-        p_forward(item)
+    for item in range(n_grp):
+        p_across(item)
+    p_relay(n_grp)
+    p_across(n_grp)
     for item in range(n_grp + 1):
         p_rest(item)
     for step in range(1, n_grp):
@@ -221,23 +244,31 @@
             device_id={"grp": target}, device_id_type=MESH,
         )
 
-    done = 0
-    for number, (start, width) in enumerate(chunks):
-        p_forward(n_grp + 1 + number)
+    ready = [0]
+
+    def finish(number):
+        start, width = chunks[number]
+        p_across(n_grp + 1 + number)
         p_rest(n_grp + 1 + number)
         ladder[:, start:start + width] = jnp.dot(
             columns, mixed[:, :, start:start + width].reshape(total, width),
             preferred_element_type=F32,
         )
-        while done < n_grp and (done + 1) * cols <= start + width:
-            block = ladder[:, done * cols:(done + 1) * cols].astype(BF16)
-            out_send[done] = block
-
-            @pl.when(grp != done)
-            def _(target=done):
+        while ready[0] < n_grp and (ready[0] + 1) * cols <= start + width:
+            target = ready[0]
+            out_send[target] = ladder[:, target * cols:(target + 1) * cols].astype(BF16)
+
+            @pl.when(grp != target)
+            def _(target=target):
                 o_copy(target, grp).start()
 
-            done += 1
+            ready[0] += 1
+
+    for number in range(len(chunks)):
+        p_relay(n_grp + 1 + number)
+        if number > 0:
+            finish(number - 1)
+    finish(len(chunks) - 1)
     for step in range(1, n_grp):
         source = peer(step)
         o_copy(source, source).wait_recv()
@@ -273,7 +304,7 @@
             pltpu.VMEM((n_grp, rows, cols), BF16),
             pltpu.VMEM((n_grp, rows, cols), BF16),
             dma((3, n_grp)), dma((3, n_grp)),
-            dma((items, n_blk)), dma((items, n_blk)),
+            dma((items, 2, n_blk)), dma((items, 2, n_blk)),
             dma((n_grp,)), dma((n_grp,)),
         ],
         compiler_params=pltpu.CompilerParams(collective_id=0, has_side_effects=True),
@@ -306,8 +337,8 @@
     def body(amplitudes, *rest):
         rows, pairs, cols = amplitudes.shape
         points, virtuals = rest[0].shape
-        fits = pairs == n_grp and n_blk & (n_blk - 1) == 0 and n_blk >= 4
-        fits = fits and rows % 16 == 0 and points % 16 == 0 and virtuals % 128 == 0
+        fits = pairs == n_grp and n_grp % 2 == 0 and n_blk == 8
+        fits = fits and rows % 16 == 0 and points % 32 == 0 and virtuals % 128 == 0
         if fits:
             return by_pair(n_blk, n_grp, amplitudes, *rest)
         return local(amplitudes, *rest)

time: 56.8 us -> 58.2 us (1.025); the launches traced: 55.7 us -> 58 us
  Pallas kernels: 49.6 us -> 51.9 us
    pallas_call x1, Pallas kernels: 49.6 us -> 51.9 us  [ladder_term(): pl.pallas_call(functools.partial(kernel, n_blk, n_grp), out_shape=jax.Sha...]
where the time goes in v2:
time: 58.2 us; the launch traced here: 58 us
  Pallas kernels  51.9 us (89%)
  local copies, waits for them, and re-layouts  4.87 us (8%)
  other arithmetic  1.16 us (2%)
    pallas_call x1, Pallas kernels, ladder_term(): pl.pallas_call(functools.partial(kernel, n_blk, n_grp), out_shape=jax.Sha...  51.9 us
    unnamed x6, local copies, waits for them, and re-layouts  2.25 us

profile of v2, /device:TPU:25, one launch (start us, length us, event | category | flops | bytes accessed | tf_op | source)
XLA Modules:
  0.0 58.0 jit_solution(17676317175785642748)
XLA Ops:
  0.0 0.0 copy-start
  0.0 0.8 %dynamic_slice.6 = f32[112]{0:T(128)S(1)} dynamic-slice(f32[896]{0:T(1024)} %param.8, s32[]{:T(128)S(6)} %select_n.6), dynamic_slice_sizes={112} | dynamic-slice | bytes 900 | tf_op jit(solution)/shard_map/dynamic_slice | solution.py:315
  0.8 0.8 %dynamic_slice.7 = f32[224]{0:T(256)S(1)} dynamic-slice(f32[896]{0:T(1024)} %param.8, s32[]{:T(128)S(6)} %select_n.7), dynamic_slice_sizes={224} | dynamic-slice | bytes 1796 | tf_op jit(solution)/shard_map/dynamic_slice | solution.py:318
  1.6 1.5 %copy.16 = bf16[128,1,256]{2,0,1:T(8,128)(2,1)} copy(f32[128,1,256]{2,1,0:T(1,128)} %param.7) | data formatting | bytes 196608 | tf_op args[2]
  3.1 0.1 broadcast_add_fusion
  3.2 0.0 copy-done
  3.2 0.7 %copy.15 = bf16[112,4,224]{2,0,1:T(8,128)(2,1)} copy(bf16[112,4,224]{2,1,0:T(4,128)(2,1)S(1)} %copy-done) | data formatting | bytes 401408 | tf_op args[0]
  3.9 0.0 copy-start.1
  3.9 51.9 %shard_map.55 = bf16[4,112,224]{2,1,0:T(8,128)(2,1)} custom-call(bf16[4,112,224]{2,1,0:T(8,128)(2,1)} %bitcast.8, bf16[32,896]{1,0:T(8,128)(2,1)} %x_ref.1, bf16[128,256]{1,0:T(8,128)(2,1)} %bitcast.9), custom_call_target="tpu_custom_call" | custom-call | tf_op jit(solution)/shard_map/pallas_call | solution.py:291
  55.8 0.0 copy-done.1
  55.8 1.1 %bitcast_add_fusion = f32[112,4,224]{2,0,1:T(8,128)S(1)} fusion(bf16[4,112,224]{2,1,0:T(8,128)(2,1)} %shard_map.55, f32[4]{0:T(128)S(1)} %copy-done.1, f32[112,224]{1,0:T(8,128)S(1)} %broadcast_add_fusion, bf16[112,4,224]{2,1,0:T(4,128)(2,1)S(1)} %copy-done), kind=kLoop, calls=%fused_computation | loop fusion | flops 501760 | bytes 903184 | tf_op jit(solution)/shard_map/add | solution.py:329
  56.9 1.1 %copy.9 = f32[112,4,224]{2,1,0:T(4,128)} copy(f32[112,4,224]{2,0,1:T(8,128)S(1)} %bitcast_add_fusion) | data formatting | bytes 802816 | tf_op jit(solution)/shard_map/add | solution.py:329
Async XLA Ops:
  0.0 3.2 %copy-start = (bf16[112,4,224]{2,1,0:T(4,128)(2,1)S(1)}, bf16[112,4,224]{2,1,0:T(4,128)(2,1)}, u32[]{:S(2)}) copy-start(bf16[112,4,224]{2,1,0:T(4,128)(2,1)} %param.5) | copy-start | bytes 602116
  3.9 51.9 %copy-start.1 = (f32[4]{0:T(128)S(1)}, f32[4]{0:T(128)}, u32[]{:S(2)}) copy-start(f32[4]{0:T(128)} %param.9) | copy-start | bytes 52

commit v3 on v2

--- a/solution.py
+++ b/solution.py
@@ -73,13 +73,13 @@
 
 
 def kernel(
-    n_blk, n_grp, t_ref, x_ref, z_ref, o_ref,
-    factor, pieces, amps, weights, left, mixed, ladder, out_send, out_recv,
-    z_send_sem, z_recv_sem, p_send_sem, p_recv_sem, o_send_sem, o_recv_sem,
+    n_blk, n_grp, t_ref, x_ref, z_ref, e_ref, f_ref, o_ref,
+    own_amps, own_weights, factor, pieces, amps, weights, left, mixed, ladder, out_send, out_recv,
+    x_send_sem, x_recv_sem, z_send_sem, z_recv_sem, p_send_sem, p_recv_sem, o_send_sem, o_recv_sem,
 ):
     me = lax.axis_index("blk")
     grp = lax.axis_index("grp")
-    pairs, rows, cols = t_ref.shape
+    rows, pairs, cols = t_ref.shape
     points, virtuals = x_ref.shape
     core, near, far = 1, 2, 4
     direct = [near, far, core]
@@ -93,10 +93,42 @@
         pl.semaphore_signal(barrier, inc=1, device_id={"grp": peer(step)}, device_id_type=MESH)
     for mask in direct:
         pl.semaphore_signal(barrier, inc=1, device_id={"blk": flip(me, mask)}, device_id_type=MESH)
+    for pair in range(pairs):
+        own_amps[pair] = t_ref[:, pair, :]
+    own_weights[...] = z_ref[:, 0, :].astype(BF16)
     pl.semaphore_wait(barrier, n_grp - 1 + len(direct))
 
     def rows_of(source, size):
         return pl.ds(pl.multiple_of(source * size, size), size)
+
+    mate, across = flip(grp, 1), n_grp - 1 - grp
+    half_index = lax.div(grp, 2)
+    inner = jnp.logical_and(grp > 0, grp < n_grp - 1)
+    owners = (grp, mate, 2 - half_index, 3 - 3 * half_index)
+
+    def x_copy(number, slot, owner, target, src=None):
+        place = factor.at[owner, rows_of(me, points), :]
+        return pltpu.make_async_remote_copy(
+            src_ref=place if src is None else src, dst_ref=place,
+            send_sem=x_send_sem.at[number], recv_sem=x_recv_sem.at[slot],
+            device_id={"grp": target}, device_id_type=MESH,
+        )
+
+    def x_wait(slot):
+        x_copy(0, slot, owners[slot], mate).wait_recv()
+
+    x_sends = (
+        lambda: x_copy(0, 1, grp, mate, x_ref),
+        lambda: x_copy(1, 2, grp, across, x_ref),
+        lambda: x_copy(2, 3, owners[1], across),
+        lambda: x_copy(3, 2, owners[2], mate),
+        lambda: x_copy(4, 3, owners[3], mate),
+    )
+
+    def x_pass(number):
+        @pl.when(inner)
+        def _():
+            x_sends[number]().start()
 
     def z_copy(kind, step, src, dst):
         return pltpu.make_async_remote_copy(
@@ -106,12 +138,10 @@
         )
 
     def z_dst(kind, source):
-        if kind == 0:
-            return factor.at[source, rows_of(me, points), :]
-        return (pieces if kind == 1 else weights).at[source]
+        return (pieces, weights)[kind].at[source]
 
     def z_start(kind, step):
-        src = (x_ref, t_ref.at[peer(step)], z_ref)[kind]
+        src = (own_amps.at[peer(step)], own_weights)[kind]
         copy = z_copy(kind, step, src, z_dst(kind, grp))
         copy.start()
         started.append(copy)
@@ -126,15 +156,16 @@
         if item < n_grp:
             part = points // 2
             begin = pl.multiple_of(source * points + half * part, part)
-            return factor.at[peer((n_grp - item) % n_grp), pl.ds(begin, part), :]
+            return factor.at[owners[item], pl.ds(begin, part), :]
         if item == n_grp:
             part = -(-rows // 32) * 16
             size = part if half == 0 else rows - part
             begin = pl.multiple_of(source * rows + half * part, 16)
             return amps.at[pl.ds(begin, size), :]
-        start, width = chunks[item - n_grp - 1]
-        part = n_grp // 2
-        return mixed.at[pl.ds(half * part, part), rows_of(source, points), pl.ds(start, width)]
+        number = item - n_grp - 1
+        part = n_grp * points // 2
+        begin = pl.multiple_of(source * 2 * part + half * part, part)
+        return mixed.at[number, pl.ds(begin, part), pl.ds(0, chunks[number][1])]
 
     def p_copy(item, half, mask, hop, src=None):
         place = region(item, half, flip(me, mask))
@@ -152,6 +183,9 @@
 
     def p_wait(item, half, mask):
         p_copy(item, half, mask, 0).wait_recv()
+
+    def relayed(item):
+        return item != n_grp + len(chunks)
 
     def p_spread(item, src=None):
         sources = (None, None)
@@ -161,6 +195,9 @@
         for turn in range(2):
             p_send(item, turn, 0, near, sources[turn])
             p_send(item, 1 - turn, 0, far, sources[1 - turn])
+        if not relayed(item):
+            for half in range(2):
+                p_send(item, half, 0, near + far, sources[half])
         for half in range(2):
             p_send(item, half, 0, core, sources[half])
 
@@ -168,7 +205,7 @@
         for turn in range(2):
             for mask, half, onward in ((near, turn, far), (far, 1 - turn, near)):
                 p_wait(item, half, mask)
-                if turn == 0:
+                if turn == 0 and relayed(item):
                     p_send(item, half, mask, onward)
                 p_send(item, half, mask, core)
 
@@ -182,33 +219,52 @@
             for half in range(2):
                 p_wait(item, half, mask)
 
+    x_sends[0]().start()
+    x_pass(1)
+    p_spread(0, x_ref)
     for step in range(1, n_grp):
         z_start(0, step)
-    p_spread(0, x_ref)
-    for kind in (1, 2):
-        for step in range(1, n_grp):
-            z_start(kind, step)
     factor[grp, rows_of(me, points), :] = x_ref[...]
-    pieces[grp] = t_ref[grp]
-    weights[grp] = z_ref[...]
+    pieces[grp] = own_amps[grp]
+    weights[grp] = own_weights[...]
+    x_wait(1)
+    x_pass(2)
+    p_spread(1)
+    p_relay(0)
+    x_wait(2)
+    x_pass(3)
+    p_spread(2)
+    p_relay(1)
+
+    @pl.when(inner)
+    def _():
+        x_wait(3)
+
+    x_pass(4)
+    for step in range(1, n_grp):
+        z_start(1, step)
     for step in range(1, n_grp):
         z_wait(0, step)
-        p_spread(step)
-        p_relay(step - 1)
-    p_relay(n_grp - 1)
-    for step in range(1, n_grp):
-        z_wait(1, step)
     for g in range(n_grp):
         amps[rows_of(me, rows), g * cols:(g + 1) * cols] = pieces[g]
     p_spread(n_grp)
-    for item in range(n_grp):
+    p_relay(2)
+
+    @pl.when(jnp.logical_not(inner))
+    def _():
+        x_wait(3)
+
+    p_spread(3)
+    for item in range(3):
         p_across(item)
     p_relay(n_grp)
+    p_relay(3)
     p_across(n_grp)
+    p_across(3)
     for item in range(n_grp + 1):
         p_rest(item)
     for step in range(1, n_grp):
-        z_wait(2, step)
+        z_wait(1, step)
 
     own = factor[:, rows_of(me, points), :].reshape(n_grp * points, virtuals)
     left[...] = jnp.dot(own, amps[...], preferred_element_type=F32).astype(BF16)
@@ -225,15 +281,28 @@
             weighted, factor[:, :, start:start + width].reshape(total, width),
             preferred_element_type=F32,
         ).astype(BF16)
-        mixed[:, rows_of(me, points), start:start + width] = part.reshape(n_grp, points, width)
+        mixed[number, rows_of(me, n_grp * points), :width] = part
         p_spread(n_grp + 1 + number)
 
     picked = lax.broadcasted_iota(jnp.int32, (rows, virtuals), 1) == (
         lax.broadcasted_iota(jnp.int32, (rows, virtuals), 0) + me * rows
     )
+    energies = e_ref[...].reshape(1, virtuals)
+    first_energy = jnp.sum(jnp.where(picked, energies, 0.0), axis=1, keepdims=True)
+    second_energy = jnp.zeros((1, cols), F32)
+    for g in range(n_grp):
+        second_energy += jnp.where(grp == g, energies[:, g * cols:(g + 1) * cols], 0.0)
+    energy_sum = first_energy + second_energy
     picked = picked.astype(F32).astype(BF16)
+    by_owner = jnp.concatenate(
+        [
+            factor[:, block * points:(block + 1) * points, :].reshape(n_grp * points, virtuals)
+            for block in range(n_blk)
+        ],
+        axis=0,
+    )
     columns = lax.dot_general(
-        picked, factor[...].reshape(total, virtuals), (((1,), (1,)), ((), ())),
+        picked, by_owner, (((1,), (1,)), ((), ())),
         preferred_element_type=F32,
     ).astype(BF16)
 
@@ -251,7 +320,7 @@
         p_across(n_grp + 1 + number)
         p_rest(n_grp + 1 + number)
         ladder[:, start:start + width] = jnp.dot(
-            columns, mixed[:, :, start:start + width].reshape(total, width),
+            columns, mixed[number, :, :width],
             preferred_element_type=F32,
         )
         while ready[0] < n_grp and (ready[0] + 1) * cols <= start + width:
@@ -264,69 +333,66 @@
 
             ready[0] += 1
 
-    for number in range(len(chunks)):
-        p_relay(n_grp + 1 + number)
-        if number > 0:
-            finish(number - 1)
-    finish(len(chunks) - 1)
-    for step in range(1, n_grp):
-        source = peer(step)
-        o_copy(source, source).wait_recv()
-        o_ref[source] = out_recv[source]
-    o_ref[grp] = out_send[grp]
+    ahead = 3
+    for number in range(len(chunks) + ahead - 1):
+        if number < len(chunks):
+            p_relay(n_grp + 1 + number)
+        if number >= ahead - 1:
+            finish(number - ahead + 1)
+    out_recv[grp] = out_send[grp]
+    for pair in range(pairs):
+        @pl.when(grp != pair)
+        def _(pair=pair):
+            o_copy(pair, pair).wait_recv()
+
+        diagonal = (energy_sum - f_ref[pair]) * own_amps[pair].astype(F32)
+        o_ref[pair] = diagonal + out_recv[pair].astype(F32)
     for target in range(n_grp):
         @pl.when(grp != target)
         def _(target=target):
             o_copy(target, grp).wait_send()
     for copy in started:
         copy.wait_send()
-
-
-def ladder_term(n_blk, n_grp, amps, factor_rows, weights):
-    pairs, rows, cols = amps.shape
-    points, virtuals = factor_rows.shape
-    items = n_grp + 1 + len(column_chunks(virtuals, -(-cols // 128) * 128))
+    x_sends[0]().wait_send()
+
+    @pl.when(inner)
+    def _():
+        for send in x_sends[1:]:
+            send().wait_send()
+
+
+def by_pair(n_blk, n_grp, amplitudes, grid_factor, metric, virt_energy, pair_energy):
+    rows, pairs, cols = amplitudes.shape
+    points, virtuals = grid_factor.shape
+    height, unused, width = metric.shape
+    chunks = column_chunks(virtuals, -(-cols // 128) * 128)
+    items = n_grp + 1 + len(chunks)
     dma = pltpu.SemaphoreType.DMA
     vmem = pl.BlockSpec(memory_space=pltpu.VMEM)
-    return pl.pallas_call(
+    residual = pl.pallas_call(
         functools.partial(kernel, n_blk, n_grp),
-        out_shape=jax.ShapeDtypeStruct(amps.shape, BF16),
-        in_specs=[vmem] * 3,
+        out_shape=jax.ShapeDtypeStruct((pairs, rows, cols), F32),
+        in_specs=[vmem] * 4 + [pl.BlockSpec(memory_space=pltpu.SMEM)],
         out_specs=vmem,
         scratch_shapes=[
+            pltpu.VMEM((pairs, rows, cols), BF16),
+            pltpu.VMEM((height, width), BF16),
             pltpu.VMEM((n_grp, n_blk * points, virtuals), BF16),
             pltpu.VMEM((n_grp, rows, cols), BF16),
             pltpu.VMEM((n_blk * rows, virtuals), BF16),
-            pltpu.VMEM((n_grp,) + weights.shape, BF16),
+            pltpu.VMEM((n_grp, height, width), BF16),
             pltpu.VMEM((n_grp * points, virtuals), BF16),
-            pltpu.VMEM((n_grp, n_blk * points, virtuals), BF16),
+            pltpu.VMEM((len(chunks), n_grp * n_blk * points, chunks[0][1]), BF16),
             pltpu.VMEM((rows, virtuals), F32),
             pltpu.VMEM((n_grp, rows, cols), BF16),
             pltpu.VMEM((n_grp, rows, cols), BF16),
-            dma((3, n_grp)), dma((3, n_grp)),
+            dma((5,)), dma((4,)), dma((2, n_grp)), dma((2, n_grp)),
             dma((items, 2, n_blk)), dma((items, 2, n_blk)),
             dma((n_grp,)), dma((n_grp,)),
         ],
         compiler_params=pltpu.CompilerParams(collective_id=0, has_side_effects=True),
-    )(amps, factor_rows, weights)
-
-
-def denominators(amplitudes, virt_energy, pair_energy):
-    first_energy = lax.dynamic_slice_in_dim(
-        virt_energy, lax.axis_index("blk") * amplitudes.shape[0], amplitudes.shape[0]
-    )
-    second_energy = lax.dynamic_slice_in_dim(
-        virt_energy, lax.axis_index("grp") * amplitudes.shape[2], amplitudes.shape[2]
-    )
-    return first_energy[:, None, None] + second_energy[None, None, :] - pair_energy[None, :, None]
-
-
-def by_pair(n_blk, n_grp, amplitudes, grid_factor, metric, virt_energy, pair_energy):
-    ladder = ladder_term(
-        n_blk, n_grp, jnp.transpose(amplitudes, (1, 0, 2)), grid_factor, metric[:, 0].astype(BF16)
-    )
-    denominator = denominators(amplitudes, virt_energy, pair_energy)
-    return denominator * amplitudes.astype(F32) + jnp.transpose(ladder, (1, 0, 2)).astype(F32)
+    )(amplitudes, grid_factor, metric, virt_energy, pair_energy)
+    return jnp.transpose(residual, (1, 0, 2))
 
 
 def solution(mesh):
@@ -337,7 +403,7 @@
     def body(amplitudes, *rest):
         rows, pairs, cols = amplitudes.shape
         points, virtuals = rest[0].shape
-        fits = pairs == n_grp and n_grp % 2 == 0 and n_blk == 8
+        fits = pairs == n_grp and n_grp == 4 and n_blk == 8
         fits = fits and rows % 16 == 0 and points % 32 == 0 and virtuals % 128 == 0
         if fits:
             return by_pair(n_blk, n_grp, amplitudes, *rest)

time: 58.2 us -> 52.1 us (0.90); the launches traced: 58 us -> 51 us
  Pallas kernels: 51.9 us -> 49 us
  local copies, waits for them, and re-layouts: 4.87 us -> 2.08 us
  other arithmetic: 1.16 us -> 0 us
    pallas_call x1, Pallas kernels: 51.9 us -> 49 us  [by_pair(): pl.pallas_call(functools.partial(kernel, n_blk, n_grp), out_shape=jax.Sha...]
    unnamed x6 -> x0, local copies, waits for them, and re-layouts: 2.25 us -> none
    transpose x0 -> x1, local copies, waits for them, and re-layouts: none -> 2.08 us  [by_pair(): return jnp.transpose(residual, (1, 0, 2))]
    dynamic_slice x2 -> x0, local copies, waits for them, and re-layouts: 1.56 us -> none  [the longest x1 0.8 us: denominators(): lax.dynamic_slice_in_dim(virt_energy, lax.axis_index('blk') * amplitudes....]
    add x2 -> x0, other arithmetic: 1.16 us -> none  [the longest x1 1.08 us: by_pair(): denominator * amplitudes.astype(F32)]
    add x1 -> x0, local copies, waits for them, and re-layouts: 1.06 us -> none  [by_pair(): denominator * amplitudes.astype(F32)]
where the time goes in v3:
time: 52.1 us; the launch traced here: 51 us
  Pallas kernels  49 us (94%)
  local copies, waits for them, and re-layouts  2.08 us (4%)
    pallas_call x1, Pallas kernels, by_pair(): pl.pallas_call(functools.partial(kernel, n_blk, n_grp), out_shape=jax.Sha...  49 us
    transpose x1, local copies, waits for them, and re-layouts, by_pair(): return jnp.transpose(residual, (1, 0, 2))  2.08 us

profile of v3, /device:TPU:25, one launch (start us, length us, event | category | flops | bytes accessed | tf_op | source)
XLA Modules:
  0.0 51.0 jit_solution(9303685190694358881)
XLA Ops:
  0.0 49.0 %shard_map.55 = f32[4,112,224]{2,1,0:T(8,128)} custom-call(bf16[112,4,224]{2,1,0:T(4,128)(2,1)} %t_ref.1, bf16[32,896]{1,0:T(8,128)(2,1)} %x_ref.1, f32[128,1,256]{2,1,0:T(1,128)} %z_ref.1, f32[896]{0:T(1024)} %e_ref.1, f32[4]{0:T(128)} %f_ref.1), custom_call_target="tpu_custom_call" | custom-call | tf_op jit(solution)/shard_map/pallas_call | solution.py:372
  49.0 2.1 %copy.6 = f32[112,4,224]{2,1,0:T(4,128)} copy(f32[112,4,224]{2,0,1:T(8,128)} %bitcast.1) | data formatting | bytes 802816 | tf_op jit(solution)/shard_map/transpose | solution.py:395

commit v4 on v3

--- a/solution.py
+++ b/solution.py
@@ -73,9 +73,9 @@
 
 
 def kernel(
-    n_blk, n_grp, t_ref, x_ref, z_ref, e_ref, f_ref, o_ref,
-    own_amps, own_weights, factor, pieces, amps, weights, left, mixed, ladder, out_send, out_recv,
-    x_send_sem, x_recv_sem, z_send_sem, z_recv_sem, p_send_sem, p_recv_sem, o_send_sem, o_recv_sem,
+    n_blk, n_grp, t_hbm, x_hbm, z_hbm, e_ref, f_ref, o_ref,
+    t_ref, x_ref, z_ref, in_sem, own_amps, own_weights, factor, pieces, amps, weights, left, mixed, ladder, out_send, out_recv,
+    z_send_sem, z_recv_sem, p_send_sem, p_recv_sem, o_send_sem, o_recv_sem,
 ):
     me = lax.axis_index("blk")
     grp = lax.axis_index("grp")
@@ -86,49 +86,34 @@
     started = []
 
     def peer(step):
-        return lax.rem(grp + step, n_grp)
+        return flip(grp, step)
 
     barrier = pltpu.get_barrier_semaphore()
+    loads = [
+        pltpu.make_async_copy(src, dst, in_sem.at[number])
+        for number, (src, dst) in enumerate(
+            ((t_hbm, t_ref), (z_hbm, z_ref), (x_hbm, x_ref))
+        )
+    ]
+    for load in loads:
+        load.start()
     for step in range(1, n_grp):
         pl.semaphore_signal(barrier, inc=1, device_id={"grp": peer(step)}, device_id_type=MESH)
     for mask in direct:
         pl.semaphore_signal(barrier, inc=1, device_id={"blk": flip(me, mask)}, device_id_type=MESH)
+    loads[0].wait()
     for pair in range(pairs):
         own_amps[pair] = t_ref[:, pair, :]
+    for load in loads[1:]:
+        load.wait()
     own_weights[...] = z_ref[:, 0, :].astype(BF16)
     pl.semaphore_wait(barrier, n_grp - 1 + len(direct))
 
     def rows_of(source, size):
         return pl.ds(pl.multiple_of(source * size, size), size)
 
-    mate, across = flip(grp, 1), n_grp - 1 - grp
-    half_index = lax.div(grp, 2)
-    inner = jnp.logical_and(grp > 0, grp < n_grp - 1)
-    owners = (grp, mate, 2 - half_index, 3 - 3 * half_index)
-
-    def x_copy(number, slot, owner, target, src=None):
-        place = factor.at[owner, rows_of(me, points), :]
-        return pltpu.make_async_remote_copy(
-            src_ref=place if src is None else src, dst_ref=place,
-            send_sem=x_send_sem.at[number], recv_sem=x_recv_sem.at[slot],
-            device_id={"grp": target}, device_id_type=MESH,
-        )
-
-    def x_wait(slot):
-        x_copy(0, slot, owners[slot], mate).wait_recv()
-
-    x_sends = (
-        lambda: x_copy(0, 1, grp, mate, x_ref),
-        lambda: x_copy(1, 2, grp, across, x_ref),
-        lambda: x_copy(2, 3, owners[1], across),
-        lambda: x_copy(3, 2, owners[2], mate),
-        lambda: x_copy(4, 3, owners[3], mate),
-    )
-
-    def x_pass(number):
-        @pl.when(inner)
-        def _():
-            x_sends[number]().start()
+    cut = -(-rows // 32) * 16
+    groups = ((0, cut), (cut, rows - cut))
 
     def z_copy(kind, step, src, dst):
         return pltpu.make_async_remote_copy(
@@ -138,31 +123,42 @@
         )
 
     def z_dst(kind, source):
-        return (pieces, weights)[kind].at[source]
+        if kind == 0:
+            return factor.at[source, rows_of(me, points), :]
+        if kind == 3:
+            return weights.at[source]
+        begin, size = groups[kind - 1]
+        return pieces.at[source, begin:begin + size, :]
 
     def z_start(kind, step):
-        src = (own_amps.at[peer(step)], own_weights)[kind]
+        if kind in (1, 2):
+            begin, size = groups[kind - 1]
+            src = own_amps.at[peer(step), begin:begin + size, :]
+        else:
+            src = x_ref if kind == 0 else own_weights
         copy = z_copy(kind, step, src, z_dst(kind, grp))
         copy.start()
         started.append(copy)
 
     def z_wait(kind, step):
-        dst = z_dst(kind, peer(n_grp - step))
+        dst = z_dst(kind, peer(step))
         z_copy(kind, step, dst, dst).wait_recv()
 
     chunks = column_chunks(virtuals, -(-cols // 128) * 128)
+
+    first = n_grp + len(groups)
 
     def region(item, half, source):
         if item < n_grp:
             part = points // 2
             begin = pl.multiple_of(source * points + half * part, part)
-            return factor.at[owners[item], pl.ds(begin, part), :]
-        if item == n_grp:
-            part = -(-rows // 32) * 16
-            size = part if half == 0 else rows - part
-            begin = pl.multiple_of(source * rows + half * part, 16)
-            return amps.at[pl.ds(begin, size), :]
-        number = item - n_grp - 1
+            return factor.at[peer(item), pl.ds(begin, part), :]
+        if item < first:
+            begin, size = groups[item - n_grp]
+            part = -(-size // 32) * 16
+            begin += half * part + source * rows
+            return amps.at[pl.ds(pl.multiple_of(begin, 16), part if half == 0 else size - part), :]
+        number = item - first
         part = n_grp * points // 2
         begin = pl.multiple_of(source * 2 * part + half * part, part)
         return mixed.at[number, pl.ds(begin, part), pl.ds(0, chunks[number][1])]
@@ -185,7 +181,7 @@
         p_copy(item, half, mask, 0).wait_recv()
 
     def relayed(item):
-        return item != n_grp + len(chunks)
+        return item != first + len(chunks) - 1
 
     def p_spread(item, src=None):
         sources = (None, None)
@@ -219,52 +215,43 @@
             for half in range(2):
                 p_wait(item, half, mask)
 
-    x_sends[0]().start()
-    x_pass(1)
     p_spread(0, x_ref)
-    for step in range(1, n_grp):
-        z_start(0, step)
+    z_start(0, 1)
+    for kind in (1, 2):
+        for step in (1, 2, 3):
+            z_start(kind, step)
+    z_start(0, 3)
+    z_start(0, 2)
+    for step in (1, 2, 3):
+        z_start(3, step)
     factor[grp, rows_of(me, points), :] = x_ref[...]
     pieces[grp] = own_amps[grp]
     weights[grp] = own_weights[...]
-    x_wait(1)
-    x_pass(2)
+    z_wait(0, 1)
     p_spread(1)
     p_relay(0)
-    x_wait(2)
-    x_pass(3)
-    p_spread(2)
-    p_relay(1)
-
-    @pl.when(inner)
-    def _():
-        x_wait(3)
-
-    x_pass(4)
-    for step in range(1, n_grp):
-        z_start(1, step)
-    for step in range(1, n_grp):
+    for number, (begin, size) in enumerate(groups):
+        for step in (1, 2, 3):
+            z_wait(1 + number, step)
+        place = pl.ds(pl.multiple_of(me * rows + begin, 16), size)
+        for g in range(n_grp):
+            amps[place, g * cols:(g + 1) * cols] = pieces[g, begin:begin + size, :]
+        p_spread(n_grp + number)
+        p_relay(1 if number == 0 else n_grp)
+    for step in (3, 2):
         z_wait(0, step)
-    for g in range(n_grp):
-        amps[rows_of(me, rows), g * cols:(g + 1) * cols] = pieces[g]
-    p_spread(n_grp)
+        p_spread(step)
+    p_relay(n_grp + 1)
+    p_relay(3)
+    for item in (0, 1, n_grp):
+        p_across(item)
     p_relay(2)
-
-    @pl.when(jnp.logical_not(inner))
-    def _():
-        x_wait(3)
-
-    p_spread(3)
-    for item in range(3):
+    for item in (n_grp + 1, 3, 2):
         p_across(item)
-    p_relay(n_grp)
-    p_relay(3)
-    p_across(n_grp)
-    p_across(3)
-    for item in range(n_grp + 1):
+    for item in range(first):
         p_rest(item)
-    for step in range(1, n_grp):
-        z_wait(1, step)
+    for step in (1, 2, 3):
+        z_wait(3, step)
 
     own = factor[:, rows_of(me, points), :].reshape(n_grp * points, virtuals)
     left[...] = jnp.dot(own, amps[...], preferred_element_type=F32).astype(BF16)
@@ -282,7 +269,7 @@
             preferred_element_type=F32,
         ).astype(BF16)
         mixed[number, rows_of(me, n_grp * points), :width] = part
-        p_spread(n_grp + 1 + number)
+        p_spread(first + number)
 
     picked = lax.broadcasted_iota(jnp.int32, (rows, virtuals), 1) == (
         lax.broadcasted_iota(jnp.int32, (rows, virtuals), 0) + me * rows
@@ -317,8 +304,8 @@
 
     def finish(number):
         start, width = chunks[number]
-        p_across(n_grp + 1 + number)
-        p_rest(n_grp + 1 + number)
+        p_across(first + number)
+        p_rest(first + number)
         ladder[:, start:start + width] = jnp.dot(
             columns, mixed[number, :, :width],
             preferred_element_type=F32,
@@ -336,7 +323,7 @@
     ahead = 3
     for number in range(len(chunks) + ahead - 1):
         if number < len(chunks):
-            p_relay(n_grp + 1 + number)
+            p_relay(first + number)
         if number >= ahead - 1:
             finish(number - ahead + 1)
     out_recv[grp] = out_send[grp]
@@ -353,12 +340,6 @@
             o_copy(target, grp).wait_send()
     for copy in started:
         copy.wait_send()
-    x_sends[0]().wait_send()
-
-    @pl.when(inner)
-    def _():
-        for send in x_sends[1:]:
-            send().wait_send()
 
 
 def by_pair(n_blk, n_grp, amplitudes, grid_factor, metric, virt_energy, pair_energy):
@@ -366,15 +347,19 @@
     points, virtuals = grid_factor.shape
     height, unused, width = metric.shape
     chunks = column_chunks(virtuals, -(-cols // 128) * 128)
-    items = n_grp + 1 + len(chunks)
+    items = n_grp + 2 + len(chunks)
     dma = pltpu.SemaphoreType.DMA
     vmem = pl.BlockSpec(memory_space=pltpu.VMEM)
     residual = pl.pallas_call(
         functools.partial(kernel, n_blk, n_grp),
         out_shape=jax.ShapeDtypeStruct((pairs, rows, cols), F32),
-        in_specs=[vmem] * 4 + [pl.BlockSpec(memory_space=pltpu.SMEM)],
+        in_specs=[pl.BlockSpec(memory_space=pltpu.HBM)] * 3 + [vmem, pl.BlockSpec(memory_space=pltpu.SMEM)],
         out_specs=vmem,
         scratch_shapes=[
+            pltpu.VMEM(amplitudes.shape, BF16),
+            pltpu.VMEM(grid_factor.shape, BF16),
+            pltpu.VMEM(metric.shape, F32),
+            dma((3,)),
             pltpu.VMEM((pairs, rows, cols), BF16),
             pltpu.VMEM((height, width), BF16),
             pltpu.VMEM((n_grp, n_blk * points, virtuals), BF16),
@@ -386,7 +371,7 @@
             pltpu.VMEM((rows, virtuals), F32),
             pltpu.VMEM((n_grp, rows, cols), BF16),
             pltpu.VMEM((n_grp, rows, cols), BF16),
-            dma((5,)), dma((4,)), dma((2, n_grp)), dma((2, n_grp)),
+            dma((4, n_grp)), dma((4, n_grp)),
             dma((items, 2, n_blk)), dma((items, 2, n_blk)),
             dma((n_grp,)), dma((n_grp,)),
         ],

time: 52.1 us -> 50.6 us (0.971)
  Pallas kernels: 49 us -> 47.9 us
    pallas_call x1, Pallas kernels: 49 us -> 47.9 us  [by_pair(): pl.pallas_call(functools.partial(kernel, n_blk, n_grp), out_shape=jax.Sha...]
where the time goes in v4:
time: 50.6 us; the launch traced here: 50 us
  Pallas kernels  47.9 us (95%)
  local copies, waits for them, and re-layouts  2.08 us (4%)
    pallas_call x1, Pallas kernels, by_pair(): pl.pallas_call(functools.partial(kernel, n_blk, n_grp), out_shape=jax.Sha...  47.9 us
    transpose x1, local copies, waits for them, and re-layouts, by_pair(): return jnp.transpose(residual, (1, 0, 2))  2.08 us

profile of v4, /device:TPU:25, one launch (start us, length us, event | category | flops | bytes accessed | tf_op | source)
XLA Modules:
  0.0 50.0 jit_solution(14353856382709407944)
XLA Ops:
  0.0 47.9 %shard_map.55 = f32[4,112,224]{2,1,0:T(8,128)} custom-call(bf16[112,4,224]{2,1,0:T(4,128)(2,1)} %t_hbm.1, bf16[32,896]{1,0:T(8,128)(2,1)} %x_hbm.1, f32[128,1,256]{2,1,0:T(1,128)} %z_hbm.1, f32[896]{0:T(1024)} %e_ref.1, f32[4]{0:T(128)} %f_ref.1), custom_call_target="tpu_custom_call" | custom-call | tf_op jit(solution)/shard_map/pallas_call | solution.py:353
  47.9 2.1 %copy.6 = f32[112,4,224]{2,1,0:T(4,128)} copy(f32[112,4,224]{2,0,1:T(8,128)} %bitcast.1) | data formatting | bytes 802816 | tf_op jit(solution)/shard_map/transpose | solution.py:380

commit v5 on v4

--- a/solution.py
+++ b/solution.py
@@ -181,7 +181,7 @@
         p_copy(item, half, mask, 0).wait_recv()
 
     def relayed(item):
-        return item != first + len(chunks) - 1
+        return item not in (2, first + len(chunks) - 1)
 
     def p_spread(item, src=None):
         sources = (None, None)
@@ -320,7 +320,7 @@
 
             ready[0] += 1
 
-    ahead = 3
+    ahead = 4
     for number in range(len(chunks) + ahead - 1):
         if number < len(chunks):
             p_relay(first + number)

time: 50.6 us -> 50.1 us (level)
  no operation moved by 1% of the time
where the time goes in v5:
time: 50.1 us; the launch traced here: 49.9 us
  Pallas kernels  47.8 us (95%)
  local copies, waits for them, and re-layouts  2.08 us (4%)
    pallas_call x1, Pallas kernels, by_pair(): pl.pallas_call(functools.partial(kernel, n_blk, n_grp), out_shape=jax.Sha...  47.8 us
    transpose x1, local copies, waits for them, and re-layouts, by_pair(): return jnp.transpose(residual, (1, 0, 2))  2.08 us

profile of v5, /device:TPU:25, one launch (start us, length us, event | category | flops | bytes accessed | tf_op | source)
XLA Modules:
  0.0 49.9 jit_solution(7269270011410055317)
XLA Ops:
  0.0 47.8 %shard_map.55 = f32[4,112,224]{2,1,0:T(8,128)} custom-call(bf16[112,4,224]{2,1,0:T(4,128)(2,1)} %t_hbm.1, bf16[32,896]{1,0:T(8,128)(2,1)} %x_hbm.1, f32[128,1,256]{2,1,0:T(1,128)} %z_hbm.1, f32[896]{0:T(1024)} %e_ref.1, f32[4]{0:T(128)} %f_ref.1), custom_call_target="tpu_custom_call" | custom-call | tf_op jit(solution)/shard_map/pallas_call | solution.py:353
  47.8 2.1 %copy.6 = f32[112,4,224]{2,1,0:T(4,128)} copy(f32[112,4,224]{2,0,1:T(8,128)} %bitcast.1) | data formatting | bytes 802816 | tf_op jit(solution)/shard_map/transpose | solution.py:380
